TPU v7x, 32 devices: a whole 2x2x4 slice. The times are simulated.
32 devices in a mesh: dp: 16 (over z, y, x), layer: 2 (over core).
Axes of the slice: x: 2, y: 2, z: 4, core: 2. Of those that a mesh axis runs over, the one named last changes fastest.
Arguments:
- layer_inputs: bfloat16 [2, 16384, 4096], P('layer', 'dp'), may hold values from -6 to 6
- output_grads: bfloat16 [2, 16384, 512], P('layer', 'dp'), may hold values from -6 to 6
- input_factors: bfloat16 [128, 2, 4, 4096], P('dp', 'layer'), may hold values from -0.09375 to 0.09375
- output_factors: bfloat16 [128, 2, 4, 512], P('dp', 'layer'), may hold values from -0.25 to 0.25
Outputs:
- scores: float32 [128, 16384], P(None, 'dp')
All inputs are finite; a program needn't handle non-finite values.
Results may differ from a plain program's by a relative error of at most 0.0003.
Values may be sent and summed in bfloat16 or wider, within the bound.
A program may use at most 128 MiB of HBM per device.

v0:
```python
import jax
import jax.numpy as jnp
from jax import lax
from jax.sharding import PartitionSpec as P


def layer_term(acts, grads, in_fac, out_fac):
    count = in_fac.shape[0]
    in_flat = in_fac.reshape(count * in_fac.shape[1], in_fac.shape[2])
    out_flat = out_fac.reshape(count * out_fac.shape[1], out_fac.shape[2])
    proj_in = lax.dot_general(
        acts, in_flat, (((1,), (1,)), ((), ())), preferred_element_type=jnp.float32
    )
    proj_out = lax.dot_general(
        grads, out_flat, (((1,), (1,)), ((), ())), preferred_element_type=jnp.float32
    )
    joined = (proj_in * proj_out).reshape(acts.shape[0], count, in_fac.shape[1])
    return jnp.sum(joined, axis=2).T


def local_scores(layer_inputs, output_grads, in_piece, out_piece):
    term = layer_term(layer_inputs[0], output_grads[0], in_piece[:, 0], out_piece[:, 0])
    return term


def shards(layer_inputs, output_grads, input_factors, output_factors):
    in_all, out_all = (
        lax.all_gather(input_factors, "dp", axis=0, tiled=True),
        lax.all_gather(output_factors, "dp", axis=0, tiled=True),
    )
    partial_scores = local_scores(layer_inputs, output_grads, in_all, out_all)
    share = lax.psum_scatter(partial_scores, "layer", scatter_dimension=0, tiled=True)
    return lax.all_gather(share, "layer", axis=0, tiled=True)


def solution(mesh):
    in_specs = (
        P("layer", "dp", None),
        P("layer", "dp", None),
        P("dp", "layer", None, None),
        P("dp", "layer", None, None),
    )
    out_specs = P(None, "dp")
    return jax.shard_map(shards, mesh=mesh, in_specs=in_specs, out_specs=out_specs, check_vma=False)
```

profile of v0, /device:TPU:0, one launch (start us, length us, event | category | flops | bytes accessed | tf_op | source)
XLA Modules:
  0.0 127.8 jit_solution(10601919179193906589)
XLA Ops:
  6.5 0.0 copy-start
  6.5 0.0 all-gather.2.cloned.1.call-start
  6.5 0.7 all-gather.2.cloned.1.call-update
  7.3 0.0 reduce-scatter.2.cloned.1.call-start
  7.3 46.7 %all_gather.10 = bf16[128,1,4,512]{3,2,1,0:T(4,128)(2,1)S(1)} all-gather(bf16[8,1,4,512]{3,2,1,0:T(4,128)(2,1)} %param.7), channel_id=1, replica_groups=mesh['dp'=16,'layer'=2] {'dp'}, dimensions={0}, use_global_device_ids=true | all-gather | bytes 557056 | tf_op jit(solution)/shard_map/all_gather | solution.py:29
  54.0 0.1 reshape_squeeze.7
  54.1 35.7 %all-gather.2.cloned.1.call-done = bf16[128,1,4,4096]{3,2,1,0:T(4,128)(2,1)} async-done(((bf16[8,1,4,4096]{3,2,1,0:T(4,128)(2,1)}), bf16[128,1,4,4096]{3,2,1,0:T(4,128)(2,1)}) %all-gather.2.cloned.1.call-update) | async-done | bytes 4194320 | tf_op jit(solution)/shard_map/all_gather | solution.py:28
  89.8 6.9 %reshape_squeeze.6 = bf16[512,4096]{1,0:T(8,128)(2,1)} reshape(bf16[128,1,4,4096]{3,2,1,0:T(4,128)(2,1)} %all-gather.2.cloned.1.call-done) | data formatting | bytes 8388608 | tf_op jit(solution)/shard_map/reshape;squeeze | solution.py:9
  96.7 8.2 %fusion = f32[1024,512]{0,1:T(8,128)S(1)} fusion(bf16[512,4096]{1,0:T(8,128)(2,1)} %reshape_squeeze.6, bf16[1,1024,4096]{2,1,0:T(8,128)(2,1)} %param.4), kind=kOutput, calls=%fused_computation | convolution fusion | flops 4294967296 | bytes 14680064 | tf_op jit(solution)/shard_map/dot_general | solution.py:11
  104.9 0.0 copy-done
  104.9 2.1 %convolution_multiply_fusion = f32[1024,512]{0,1:T(8,128)} fusion(f32[1024,512]{0,1:T(8,128)S(1)} %fusion, bf16[512,512]{1,0:T(8,128)(2,1)S(1)} %reshape_squeeze.7, bf16[1,1024,512]{2,1,0:T(8,128)(2,1)S(1)} %copy-done), kind=kOutput, calls=%fused_computation.2 | convolution fusion | flops 537395200 | bytes 5767168 | tf_op jit(solution)/shard_map/dot_general | solution.py:14
  107.0 1.9 %reshape.3 = f32[1024,128,4]{0,2,1:T(4,128)S(1)} reshape(f32[1024,512]{0,1:T(8,128)} %convolution_multiply_fusion) | data formatting | bytes 4194304 | tf_op jit(solution)/shard_map/reshape | solution.py:17
  108.9 2.2 %reduce_sum.9 = f32[1024,128]{0,1:T(8,128)} reduce(f32[1024,128,4]{0,2,1:T(4,128)S(1)} %reshape.3, f32[]{:T(128)} %constant.0.clone.1), dimensions={2}, to_apply=%region_0.0 | reduce | flops 393216 | bytes 2621444 | tf_op jit(solution)/shard_map/reduce_sum | solution.py:18
  111.1 0.0 reduce-scatter.2.cloned.1.call-update
  111.1 6.7 %reduce-scatter.2.cloned.1.call-done = f32[64,1024]{1,0:T(8,128)} async-done(((f32[128,1024]{1,0:T(8,128)}), f32[64,1024]{1,0:T(8,128)}) %reduce-scatter.2.cloned.1.call-update) | async-done | bytes 262160 | tf_op jit(solution)/shard_map/reduce_scatter | solution.py:32
  117.8 2.4 %all_gather.11 = f32[128,1024]{1,0:T(8,128)S(1)} all-gather(f32[64,1024]{1,0:T(8,128)} %reduce-scatter.2.cloned.1.call-done), channel_id=1, replica_groups=mesh['dp'=16,'layer'=2] {'layer'}, dimensions={0}, use_global_device_ids=true | all-gather | bytes 786432 | tf_op jit(solution)/shard_map/all_gather | solution.py:33
  120.2 0.8 copy.6
Async XLA Ops:
  6.5 98.4 %copy-start = (bf16[1,1024,512]{2,1,0:T(8,128)(2,1)S(1)}, bf16[1,1024,512]{2,1,0:T(8,128)(2,1)}, u32[]{:S(2)}) copy-start(bf16[1,1024,512]{2,1,0:T(8,128)(2,1)} %param.5) | copy-start | bytes 3145732
  6.5 83.2 %all-gather.2.cloned.1.call-start = ((), (), s32[]{:S(2)}) async-start(), calls=%async_computation.1 | async-start | bytes 4456448 | tf_op jit(solution)/shard_map/all_gather | solution.py:28
  7.3 110.5 %reduce-scatter.2.cloned.1.call-start = ((), (), s32[]{:S(2)}) async-start(), calls=%async_computation.2 | async-start | bytes 786432 | tf_op jit(solution)/shard_map/reduce_scatter | solution.py:32
Sparse Core Ops, SparseCore 0:
  10.1 79.6 all-gather.1
  111.2 6.5 reduce-scatter.1
where the time goes:
time: 128 us
  blocking collectives  49.1 us (38%)
  waiting for transfers between devices  43.1 us (34%)
  between operations  13.4 us (10%)
  matrix products  10.3 us (8%)
  local copies, waits for them, and re-layouts  9.7 us (8%)
  other arithmetic  2.2 us (2%)
    all_gather x1, blocking collectives, shards(): lax.all_gather(output_factors, 'dp', axis=0, tiled=True)  46.7 us
    all_gather x1, waiting for transfers between devices, shards(): lax.all_gather(input_factors, 'dp', axis=0, tiled=True)  35.7 us
    dot_general x1, matrix products, layer_term(): lax.dot_general(acts, in_flat, (((1,), (1,)), ((), ())), preferred_elemen...  8.21 us
    another operation x1, local copies, waits for them, and re-layouts, layer_term(): in_flat = in_fac.reshape(count * in_fac.shape[1], in_fac.shape[2])  6.92 us
    reduce_scatter x1, waiting for transfers between devices, shards(): lax.psum_scatter(partial_scores, 'layer', scatter_dimension=0, tiled=True)  6.68 us
  transfers between devices with their start and end apart: 2, of which 2 were waited for; matrix products, arithmetic and copies ran while one was open for 0% of the time, Pallas kernels for 0%

commit v1 on v0

v1 whole, which is shorter than its diff:
```python
import functools

import jax
import jax.numpy as jnp
from jax import lax
from jax.experimental import pallas as pl
from jax.experimental.pallas import tpu as pltpu
from jax.sharding import PartitionSpec as P

MESH = pl.DeviceIdType.MESH
OWN, ACROSS_X, ACROSS_Y, DIAG = range(4)
PIECES = 2


def kernel(nz, layers, count, rank, own_ref, acts_hbm, grads_hbm, out_ref,
           slots, acts, grads, parts, load_sem, recv_sem, x_sem, y_sem, z_sem, psend_sem, precv_sem):
    me = lax.axis_index("dp")
    layer = lax.axis_index("layer")
    x, y, z = me % 2, (me // 2) % 2, me // 4
    rows, width = own_ref.shape
    half = rows // PIECES
    d_in = acts.shape[1]
    tokens = acts.shape[0]
    to_x = {"dp": me + 1 - 2 * x}
    to_y = {"dp": me + 2 - 4 * y}
    to_up = {"dp": (me + 4) % (4 * nz)}
    to_down = {"dp": (me + 4 * nz - 4) % (4 * nz)}
    has_up, has_down = z < nz - 1, z > 0

    load_acts = pltpu.make_async_copy(acts_hbm, acts, load_sem.at[0])
    load_grads = pltpu.make_async_copy(grads_hbm, grads, load_sem.at[1])
    load_acts.start()
    load_grads.start()

    barrier = pltpu.get_barrier_semaphore()
    pl.semaphore_signal(barrier, inc=1, device_id=to_x, device_id_type=MESH)
    pl.semaphore_signal(barrier, inc=1, device_id=to_y, device_id_type=MESH)
    for k in range(1, layers):
        pl.semaphore_signal(barrier, inc=1, device_id={"layer": (layer + k) % layers}, device_id_type=MESH)

    @pl.when(has_up)
    def _():
        pl.semaphore_signal(barrier, inc=1, device_id=to_up, device_id_type=MESH)

    @pl.when(has_down)
    def _():
        pl.semaphore_signal(barrier, inc=1, device_id=to_down, device_id_type=MESH)

    line_ends = (z + nz - 2) // (nz - 1) + (2 * nz - 3 - z) // (nz - 1)
    pl.semaphore_wait(barrier, 2 + layers - 1 + line_ends)

    def copy(src, target, level, piece, sem, device):
        at = target * nz + level
        return pltpu.make_async_remote_copy(
            src_ref=src,
            dst_ref=slots.at[at, pl.ds(piece * half, half), :],
            send_sem=sem,
            recv_sem=recv_sem.at[at, piece],
            device_id=device,
            device_id_type=MESH,
        )

    def held(source, level, piece):
        return slots.at[source * nz + level, pl.ds(piece * half, half), :]

    def arrived(target, level, piece):
        copy(held(target, level, piece), target, level, piece, x_sem.at[0, 0, 0], to_x).wait_recv()

    def mine(level, piece, first):
        return own_ref.at[pl.ds(piece * half, half), :] if first else held(OWN, level, piece)

    def up(level, piece, first):
        return copy(mine(level, piece, first), OWN, level, piece, z_sem.at[0, level, piece], to_up)

    def down(level, piece, first):
        return copy(mine(level, piece, first), OWN, level, piece, z_sem.at[1, level, piece], to_down)

    def side_x(level, piece, first):
        return copy(mine(level, piece, first), ACROSS_X, level, piece, x_sem.at[0, level, piece], to_x)

    def side_y(level, piece, first):
        return copy(mine(level, piece, first), ACROSS_Y, level, piece, y_sem.at[0, level, piece], to_y)

    def turn_x(level):
        return copy(held(ACROSS_Y, level, 0), DIAG, level, 0, x_sem.at[1, level, 0], to_x)

    def turn_y(level):
        return copy(held(ACROSS_X, level, 1), DIAG, level, 1, y_sem.at[1, level, 1], to_y)

    def at_distance(step, act):
        if step == 0:
            act(z, None)
            return

        @pl.when(z >= step)
        def _():
            act(z - step, True)

        @pl.when(z + step < nz)
        def _():
            act(z + step, False)

    def turn(level, unused):
        arrived(ACROSS_Y, level, 0)
        turn_x(level).start()
        arrived(ACROSS_X, level, 1)
        turn_y(level).start()

    for piece in range(PIECES):
        @pl.when(has_up)
        def _():
            up(z, piece, True).start()

        @pl.when(has_down)
        def _():
            down(z, piece, True).start()

        side_x(z, piece, True).start()
        side_y(z, piece, True).start()
    slots[OWN * nz + z] = own_ref[...]

    for step in range(1, nz):
        for piece in range(PIECES):
            def relay(level, from_below):
                arrived(OWN, level, piece)
                if from_below:
                    @pl.when(has_up)
                    def _():
                        up(level, piece, False).start()
                else:
                    @pl.when(has_down)
                    def _():
                        down(level, piece, False).start()
                side_x(level, piece, False).start()
                side_y(level, piece, False).start()

            at_distance(step, relay)
        at_distance(step - 1, turn)
    at_distance(nz - 1, turn)

    chunk = min(256, tokens)

    def scores_of(first, classes):
        blocks = classes * nz

        def body(i, carry):
            cols = pl.ds(pl.multiple_of(i * chunk, chunk), chunk)
            left = slots[first * nz:first * nz + blocks]
            left = left.reshape(blocks * rows, width)
            dims = (((1,), (1,)), ((), ()))
            proj_in = lax.dot_general(left[:, :d_in], acts[cols, :], dims, preferred_element_type=jnp.float32)
            proj_out = lax.dot_general(left[:, d_in:], grads[cols, :], dims, preferred_element_type=jnp.float32)
            joined = (proj_in * proj_out).reshape(blocks, rank, count, chunk)
            term = jnp.sum(joined, axis=1).reshape(blocks * count, chunk)
            parts[layer, first * nz * count:(first * nz + blocks) * count, cols] = term
            return carry

        lax.fori_loop(0, tokens // chunk, body, 0)

    def share(stage, first, classes, k):
        span = pl.ds(first * nz * count, classes * nz * count)
        return pltpu.make_async_remote_copy(
            src_ref=parts.at[layer, span, :],
            dst_ref=parts.at[layer, span, :],
            send_sem=psend_sem.at[stage, k],
            recv_sem=precv_sem.at[stage, layer],
            device_id={"layer": (layer + k) % layers},
            device_id_type=MESH,
        )

    def shared(stage, first, classes, k):
        source = (layer + k) % layers
        span = pl.ds(first * nz * count, classes * nz * count)
        pltpu.make_async_remote_copy(
            src_ref=parts.at[source, span, :],
            dst_ref=parts.at[source, span, :],
            send_sem=psend_sem.at[stage, k],
            recv_sem=precv_sem.at[stage, source],
            device_id={"layer": source},
            device_id_type=MESH,
        ).wait_recv()

    def finish(first, classes):
        for kind in range(first, first + classes):
            col = ((1 - y) if kind in (ACROSS_Y, DIAG) else y) * 2
            col = col + ((1 - x) if kind in (ACROSS_X, DIAG) else x)
            for level in range(nz):
                at = (kind * nz + level) * count
                total = parts[0, at:at + count, :]
                for other in range(1, layers):
                    total = total + parts[other, at:at + count, :]
                out_ref[pl.ds(pl.multiple_of((level * 4 + col) * count, count), count), :] = total

    for step in range(nz):
        def rest(level, unused):
            arrived(ACROSS_X, level, 0)
            arrived(ACROSS_Y, level, 1)

        at_distance(step, rest)
    load_acts.wait()
    load_grads.wait()
    scores_of(OWN, 3)
    for k in range(1, layers):
        share(0, OWN, 3, k).start()

    for step in range(nz):
        def last(level, unused):
            arrived(DIAG, level, 0)
            arrived(DIAG, level, 1)

        at_distance(step, last)
    scores_of(DIAG, 1)
    for k in range(1, layers):
        shared(0, OWN, 3, k)
    finish(OWN, 3)
    for k in range(1, layers):
        share(1, DIAG, 1, k).start()
    for k in range(1, layers):
        shared(1, DIAG, 1, k)
    finish(DIAG, 1)

    for step in range(nz):
        def sent(level, from_below):
            for piece in range(PIECES):
                if from_below is not False:
                    @pl.when(has_up)
                    def _():
                        up(level, piece, step == 0).wait_send()
                if from_below is not True:
                    @pl.when(has_down)
                    def _():
                        down(level, piece, step == 0).wait_send()
                side_x(level, piece, step == 0).wait_send()
                side_y(level, piece, step == 0).wait_send()
            turn_x(level).wait_send()
            turn_y(level).wait_send()

        at_distance(step, sent)
    for k in range(1, layers):
        share(0, OWN, 3, k).wait_send()
        share(1, DIAG, 1, k).wait_send()


def shards(nz, layers, layer_inputs, output_grads, input_factors, output_factors):
    count, _, rank, d_in = input_factors.shape
    d_out = output_factors.shape[3]
    tokens = layer_inputs.shape[1]
    rows, width = count * rank, d_in + d_out
    own = jnp.concatenate([input_factors[:, 0], output_factors[:, 0]], axis=2)
    own = jnp.swapaxes(own, 0, 1).reshape(rows, width)
    queries = 4 * nz * count
    dma = pltpu.SemaphoreType.DMA
    return pl.pallas_call(
        functools.partial(kernel, nz, layers, count, rank),
        out_shape=jax.ShapeDtypeStruct((queries, tokens), jnp.float32),
        in_specs=[
            pl.BlockSpec(memory_space=pltpu.VMEM),
            pl.BlockSpec(memory_space=pl.ANY),
            pl.BlockSpec(memory_space=pl.ANY),
        ],
        out_specs=pl.BlockSpec(memory_space=pltpu.VMEM),
        scratch_shapes=[
            pltpu.VMEM((4 * nz, rows, width), jnp.bfloat16),
            pltpu.VMEM((tokens, d_in), jnp.bfloat16),
            pltpu.VMEM((tokens, d_out), jnp.bfloat16),
            pltpu.VMEM((layers, queries, tokens), jnp.float32),
            dma((2,)),
            dma((4 * nz, PIECES)),
            dma((2, nz, PIECES)),
            dma((2, nz, PIECES)),
            dma((2, nz, PIECES)),
            dma((2, layers)),
            dma((2, layers)),
        ],
        compiler_params=pltpu.CompilerParams(
            collective_id=0, has_side_effects=True, vmem_limit_bytes=60 * 1024 * 1024
        ),
    )(own, layer_inputs[0], output_grads[0])


def solution(mesh):
    in_specs = (
        P("layer", "dp", None),
        P("layer", "dp", None),
        P("dp", "layer", None, None),
        P("dp", "layer", None, None),
    )
    body = functools.partial(shards, mesh.shape["dp"] // 4, mesh.shape["layer"])
    return jax.shard_map(body, mesh=mesh, in_specs=in_specs, out_specs=P(None, "dp"), check_vma=False)
```

time: 128 us -> 54.1 us (0.42)
  Pallas kernels: 0 us -> 50.1 us
  blocking collectives: 49.1 us -> 0 us
  waiting for transfers between devices: 43.1 us -> 0 us
  between operations: 13.4 us -> 0.01 us
  matrix products: 10.3 us -> 0 us
  local copies, waits for them, and re-layouts: 9.7 us -> 2.65 us
    pallas_call x0 -> x1, Pallas kernels: none -> 50.1 us  [shards(): pl.pallas_call(functools.partial(kernel, nz, layers, count, rank), out_sh...]
    all_gather x2 -> x0, blocking collectives: 49.1 us -> none  [the longest x1 46.7 us: shards(): lax.all_gather(output_factors, 'dp', axis=0, tiled=True)]
    all_gather x1 -> x0, waiting for transfers between devices: 35.7 us -> none  [shards(): lax.all_gather(input_factors, 'dp', axis=0, tiled=True)]
    dot_general x2 -> x0, matrix products: 10.3 us -> none  [the longest x1 8.21 us: layer_term(): lax.dot_general(acts, in_flat, (((1,), (1,)), ((), ())), preferred_elemen...]
    another operation x2 -> x0, local copies, waits for them, and re-layouts: 7.04 us -> none  [the longest x1 6.92 us: layer_term(): in_flat = in_fac.reshape(count * in_fac.shape[1], in_fac.shape[2])]
    reduce_scatter x1 -> x0, waiting for transfers between devices: 6.68 us -> none  [shards(): lax.psum_scatter(partial_scores, 'layer', scatter_dimension=0, tiled=True)]
    reduce_sum x1 -> x0, other arithmetic: 2.2 us -> none  [layer_term(): return jnp.sum(joined, axis=2).T]
    reshape x1 -> x0, local copies, waits for them, and re-layouts: 1.86 us -> none  [layer_term(): joined = (proj_in * proj_out).reshape(acts.shape[0], count, in_fac.shape[1])]
  transfers between devices with their start and end apart: 2 -> 0, of which waited for: 2 -> 0; matrix products, arithmetic and copies ran while one was open for 0% -> 0% of each run, Pallas kernels for 0% -> 0%
where the time goes in v1:
time: 54.1 us; the launch traced here: 53.8 us
  Pallas kernels  50.1 us (93%)
  local copies, waits for them, and re-layouts  2.65 us (5%)
  other arithmetic  1.1 us (2%)
    pallas_call x1, Pallas kernels, shards(): pl.pallas_call(functools.partial(kernel, nz, layers, count, rank), out_sh...  50.1 us
    unnamed x1, local copies, waits for them, and re-layouts  1.89 us
    transpose x1, other arithmetic, shards(): own = jnp.swapaxes(own, 0, 1).reshape(rows, width)  1.1 us

profile of v1, /device:TPU:0, one launch (start us, length us, event | category | flops | bytes accessed | tf_op | source)
XLA Modules:
  0.0 53.8 jit_solution(13718313518883708312)
XLA Ops:
  0.0 1.1 %maximum_bitcast_fusion = bf16[4,8,4608]{2,0,1:T(4,128)(2,1)S(1)} fusion(bf16[8,4,512]{2,1,0:T(4,128)(2,1)} %bitcast.13, bf16[8,4,4096]{2,1,0:T(4,128)(2,1)} %bitcast.12), kind=kLoop, calls=%fused_computation | loop fusion | flops 589824 | bytes 589824 | tf_op jit(solution)/shard_map/transpose | solution.py:250
  1.1 0.8 %copy.7 = bf16[4,8,4608]{2,1,0:T(8,128)(2,1)} copy(bf16[4,8,4608]{2,0,1:T(4,128)(2,1)S(1)} %maximum_bitcast_fusion) | data formatting | bytes 589824 | tf_op jit(solution)/shard_map/transpose | solution.py:250
  1.9 50.1 %shard_map.46 = f32[128,1024]{1,0:T(8,128)} custom-call(bf16[32,4608]{1,0:T(8,128)(2,1)} %bitcast.10, bf16[1024,4096]{1,0:T(8,128)(2,1)} %bitcast.9, bf16[1024,512]{1,0:T(8,128)(2,1)} %bitcast.11), custom_call_target="tpu_custom_call" | custom-call | tf_op jit(solution)/shard_map/pallas_call | solution.py:253
  52.0 1.9 %copy.9 = f32[128,1024]{1,0:T(8,128)} copy(f32[128,1024]{1,0:T(8,128)} %shard_map.46) | data formatting | bytes 1048576

commit v2 on v1

--- a/solution.py
+++ b/solution.py
@@ -9,7 +9,7 @@
 
 MESH = pl.DeviceIdType.MESH
 OWN, ACROSS_X, ACROSS_Y, DIAG = range(4)
-PIECES = 2
+PIECES = 4
 
 
 def kernel(nz, layers, count, rank, own_ref, acts_hbm, grads_hbm, out_ref,
@@ -81,11 +81,10 @@
     def side_y(level, piece, first):
         return copy(mine(level, piece, first), ACROSS_Y, level, piece, y_sem.at[0, level, piece], to_y)
 
-    def turn_x(level):
-        return copy(held(ACROSS_Y, level, 0), DIAG, level, 0, x_sem.at[1, level, 0], to_x)
-
-    def turn_y(level):
-        return copy(held(ACROSS_X, level, 1), DIAG, level, 1, y_sem.at[1, level, 1], to_y)
+    def side_turn(level, piece):
+        if piece < PIECES // 2:
+            return copy(held(ACROSS_Y, level, piece), DIAG, level, piece, x_sem.at[1, level, piece], to_x)
+        return copy(held(ACROSS_X, level, piece), DIAG, level, piece, y_sem.at[1, level, piece], to_y)
 
     def at_distance(step, act):
         if step == 0:
@@ -100,11 +99,14 @@
         def _():
             act(z + step, False)
 
-    def turn(level, unused):
-        arrived(ACROSS_Y, level, 0)
-        turn_x(level).start()
-        arrived(ACROSS_X, level, 1)
-        turn_y(level).start()
+    def turn(step, piece):
+        def act(level, unused):
+            arrived(ACROSS_Y if piece < PIECES // 2 else ACROSS_X, level, piece)
+            side_turn(level, piece).start()
+
+        at_distance(step, act)
+
+    order = [p for two in zip(range(PIECES // 2), range(PIECES // 2, PIECES)) for p in two]
 
     for piece in range(PIECES):
         @pl.when(has_up)
@@ -135,8 +137,9 @@
                 side_y(level, piece, False).start()
 
             at_distance(step, relay)
-        at_distance(step - 1, turn)
-    at_distance(nz - 1, turn)
+            turn(step - 1, order[piece])
+    for piece in order:
+        turn(nz - 1, piece)
 
     chunk = min(256, tokens)
 
@@ -193,8 +196,8 @@
 
     for step in range(nz):
         def rest(level, unused):
-            arrived(ACROSS_X, level, 0)
-            arrived(ACROSS_Y, level, 1)
+            for piece in range(PIECES):
+                arrived(ACROSS_X if piece < PIECES // 2 else ACROSS_Y, level, piece)
 
         at_distance(step, rest)
     load_acts.wait()
@@ -205,8 +208,8 @@
 
     for step in range(nz):
         def last(level, unused):
-            arrived(DIAG, level, 0)
-            arrived(DIAG, level, 1)
+            for piece in range(PIECES):
+                arrived(DIAG, level, piece)
 
         at_distance(step, last)
     scores_of(DIAG, 1)
@@ -232,8 +235,7 @@
                         down(level, piece, step == 0).wait_send()
                 side_x(level, piece, step == 0).wait_send()
                 side_y(level, piece, step == 0).wait_send()
-            turn_x(level).wait_send()
-            turn_y(level).wait_send()
+                side_turn(level, piece).wait_send()
 
         at_distance(step, sent)
     for k in range(1, layers):

time: 54.1 us -> 57.3 us (1.059)
  Pallas kernels: 50.1 us -> 53.3 us
    pallas_call x1, Pallas kernels: 50.1 us -> 53.3 us  [shards(): pl.pallas_call(functools.partial(kernel, nz, layers, count, rank), out_sh...]
where the time goes in v2:
time: 57.3 us; the launch traced here: 57 us
  Pallas kernels  53.3 us (93%)
  local copies, waits for them, and re-layouts  2.65 us (5%)
  other arithmetic  1.1 us (2%)
    pallas_call x1, Pallas kernels, shards(): pl.pallas_call(functools.partial(kernel, nz, layers, count, rank), out_sh...  53.3 us
    unnamed x1, local copies, waits for them, and re-layouts  1.89 us

profile of v2, /device:TPU:0, one launch (start us, length us, event | category | flops | bytes accessed | tf_op | source)
XLA Modules:
  0.0 57.0 jit_solution(10273609915217893392)
XLA Ops:
  0.0 1.1 %maximum_bitcast_fusion = bf16[4,8,4608]{2,0,1:T(4,128)(2,1)S(1)} fusion(bf16[8,4,512]{2,1,0:T(4,128)(2,1)} %bitcast.13, bf16[8,4,4096]{2,1,0:T(4,128)(2,1)} %bitcast.12), kind=kLoop, calls=%fused_computation | loop fusion | flops 589824 | bytes 589824 | tf_op jit(solution)/shard_map/transpose | solution.py:252
  1.1 0.8 %copy.7 = bf16[4,8,4608]{2,1,0:T(8,128)(2,1)} copy(bf16[4,8,4608]{2,0,1:T(4,128)(2,1)S(1)} %maximum_bitcast_fusion) | data formatting | bytes 589824 | tf_op jit(solution)/shard_map/transpose | solution.py:252
  1.9 53.3 %shard_map.46 = f32[128,1024]{1,0:T(8,128)} custom-call(bf16[32,4608]{1,0:T(8,128)(2,1)} %bitcast.10, bf16[1024,4096]{1,0:T(8,128)(2,1)} %bitcast.9, bf16[1024,512]{1,0:T(8,128)(2,1)} %bitcast.11), custom_call_target="tpu_custom_call" | custom-call | tf_op jit(solution)/shard_map/pallas_call | solution.py:255
  55.2 1.9 %copy.9 = f32[128,1024]{1,0:T(8,128)} copy(f32[128,1024]{1,0:T(8,128)} %shard_map.46) | data formatting | bytes 1048576
